TPU v7x, 32 devices: a whole 2x2x4 slice. The times are simulated.
32 devices in a mesh: wide: 16 (over z, x, core), narrow: 2 (over y).
Axes of the slice: x: 2, y: 2, z: 4, core: 2. Of those that a mesh axis runs over, the one named last changes fastest.
Arguments:
- right_side: float32 [3, 256, 32, 128], P(None, 'wide', 'narrow'), may hold values from -8 to 8
- occupancy: int32 [256, 32, 128], P('wide', 'narrow'), may hold values from 0 to 1, as said below
- region: int32 [256, 32, 128], P('wide', 'narrow'), may hold values from 0 to 3
- coarse_inverse: float32 [384, 384], P(('wide', 'narrow')), as said below
Outputs:
- solution_field: float32 [3, 256, 32, 128], P(None, 'wide', 'narrow')
- residual: float32 [3, 256, 32, 128], P(None, 'wide', 'narrow')
Inputs may be any that keep to these rules, and one draw needn't show every extreme that they name: `occupancy`: each subdomain has its own bone fraction between 0.15 and 0.9. `coarse_inverse`: symmetric positive definite.
All inputs are finite; a program needn't handle non-finite values.
Results may differ from a plain program's by a relative error of at most 0.00021.
Values sent between devices are 32-bit elements; how exact they have to be, the bound alone decides.
A program may use at most 64 MiB of HBM per device.

v0:
```python
import jax
import jax.numpy as jnp
from jax import lax
from jax.sharding import PartitionSpec as P

ITERS = 2


bone_stiff = 1.0
soft_stiff = 0.1


def padded_2(array, sides, width):
    for axis, dim in sides:
        count, length = (lax.axis_size(axis), array.shape[dim])
        up = [(i, (i + 1) % count) for i in range(count - 1)]
        down = [(j, i) for i, j in up]
        last = lax.slice_in_dim(array, length - width, length, axis=dim)
        first = lax.slice_in_dim(array, 0, width, axis=dim)
        before = lax.ppermute(last, axis, up)
        after = lax.ppermute(first, axis, down)
        array = jnp.concatenate([before, array, after], axis=dim)
    return array


def neighbours(padded):
    return [
        padded[..., 2:, 1:-1, 1:-1],
        padded[..., :-2, 1:-1, 1:-1],
        padded[..., 1:-1, 2:, 1:-1],
        padded[..., 1:-1, :-2, 1:-1],
        padded[..., 1:-1, 1:-1, 2:],
        padded[..., 1:-1, 1:-1, :-2],
    ]


def paired_sums(resid, precond, image):
    return lax.psum((jnp.sum(resid * precond), jnp.sum(image * precond)), ("wide", "narrow"))


def local(right_side, occupancy, region, coarse_inverse):
    stiff = soft_stiff + (bone_stiff - soft_stiff) * occupancy.astype(jnp.float32)
    stiff_pad = padded_2(stiff, (("wide", 0), ("narrow", 1)), 1)
    stiff_pad = jnp.pad(stiff_pad, ((0, 0), (0, 0), (1, 1)))
    faces = [0.5 * (stiff + other) for other in neighbours(stiff_pad)]
    diagonal = sum(faces) + 0.5 * stiff
    regions = coarse_inverse.shape[0] // 3
    onehot = (region[None] == jnp.arange(regions)[:, None, None, None]).astype(jnp.float32)

    def operate(field):
        padded = padded_2(field, (("wide", 1), ("narrow", 2)), 1)
        padded = jnp.pad(padded, ((0, 0), (0, 0), (0, 0), (1, 1)))
        result = 0.25 * stiff * (field + jnp.sum(field, axis=0, keepdims=True))
        for face, other in zip(faces, neighbours(padded)):
            result = result + face * (field - other)
        return result

    def add_rows(piece):
        return jnp.dot(coarse_inverse, piece, precision=lax.Precision.HIGHEST)

    def precondition(resid):
        coarse = jnp.einsum(
            "gxyz,cxyz->gc", onehot, resid, precision=lax.Precision.HIGHEST
        ).reshape(-1)
        answer = add_rows(lax.all_gather(coarse, ("wide", "narrow"), axis=0, tiled=True))
        spread = jnp.einsum(
            "gxyz,gc->cxyz", onehot, answer.reshape(regions, 3), precision=lax.Precision.HIGHEST
        )
        return resid / diagonal + spread

    solution = jnp.zeros_like(right_side)
    resid = right_side
    precond = precondition(resid)
    image = operate(precond)
    rz_now, product = paired_sums(resid, precond, image)
    alpha = rz_now / product
    direction, along = (precond, image)
    for step in range(ITERS):
        solution = solution + alpha * direction
        resid = resid - alpha * along
        if step + 1 < ITERS:
            precond = precondition(resid)
            image = operate(precond)
            rz_next, product = paired_sums(resid, precond, image)
            ratio = rz_next / rz_now
            alpha = rz_next / (product - ratio * rz_next / alpha)
            direction = precond + ratio * direction
            along = image + ratio * along
            rz_now = rz_next
    return (solution, resid)


def solution(mesh):
    return jax.shard_map(
        local,
        mesh=mesh,
        in_specs=(
            P(None, "wide", "narrow", None),
            P("wide", "narrow", None),
            P("wide", "narrow", None),
            P(("wide", "narrow"), None),
        ),
        out_specs=(P(None, "wide", "narrow", None), P(None, "wide", "narrow", None)),
        check_vma=False,
    )
```

profile of v0, /device:TPU:0, one launch (start us, length us, event | category | flops | bytes accessed | tf_op | source)
XLA Modules:
  0.0 233.6 jit_solution(5526013393805565769)
XLA Ops:
  0.7 1.0 multiply_add_fusion.2
  1.7 2.4 %collective-permute-start.1 = (f32[1,16,128]{2,1,0:T(8,128)S(1)}, f32[1,16,128]{2,1,0:T(8,128)S(1)}, u32[]{:S(2)}, u32[]{:S(2)}) collective-permute-start(f32[1,16,128]{2,1,0:T(8,128)S(1)} %get-tuple-element.32), channel_id=1, source_target_pairs={{0,2},{2,4},{4,6},{6,8},{8,10},{10,12},{12,14},{14,16},{16,18},{18... | collective-permute-start | bytes 24584 | tf_op jit(solution)/shard_map/ppermute | solution.py:20
  4.1 1.4 collective-permute-start
  5.5 2.5 %convolution_bitcast_fusion.1 = f32[4,3]{1,0:T(4,128)S(1)} fusion(f32[3,16,16,128]{3,2,1,0:T(8,128)} %param.4, s32[16,16,128]{2,1,0:T(8,128)} %param.6), kind=kOutput, calls=%fused_computation.20 | convolution fusion | flops 4849664 | bytes 524336 | tf_op jit(solution)/shard_map/gxyz,cxyz->gc/dot_general | solution.py:62
  8.3 43.8 %all-reduce.3 = f32[384]{0:T(512)S(1)} all-reduce(f32[384]{0:T(512)S(1)} %dynamic-update-slice), channel_id=1, replica_groups=mesh['wide'=16,'narrow'=2] {'wide','narrow'}, use_global_device_ids=true, to_apply=%add.3 | all-reduce | flops 384 | bytes 3072
  52.2 4.2 %collective-permute-start.3 = (f32[18,1,128]{2,1,0:T(1,128)S(1)}, f32[18,1,128]{2,1,0:T(1,128)S(1)}, u32[]{:S(2)}, u32[]{:S(2)}) collective-permute-start(f32[18,1,128]{2,1,0:T(1,128)S(1)} %get-tuple-element.27), channel_id=1, source_target_pairs={{0,1},{2,3},{4,5},{6,7},{8,9},{10,11},{12,13},{14,15},{16,17},{18,... | collective-permute-start | bytes 27656 | tf_op jit(solution)/shard_map/ppermute | solution.py:20
  56.4 1.3 collective-permute-start.2
  57.9 4.0 %collective-permute-done.2 = f32[18,1,128]{2,1,0:T(1,128)S(1)} collective-permute-done((f32[18,1,128]{2,1,0:T(1,128)S(1)}, f32[18,1,128]{2,1,0:T(1,128)S(1)}, u32[]{:S(2)}, u32[]{:S(2)}) %collective-permute-start.2) | collective-permute-done | bytes 9248 | tf_op jit(solution)/shard_map/ppermute | solution.py:21
  62.4 1.0 convolution_add_fusion.1
  63.4 1.3 collective-permute-start.5
  64.7 1.3 collective-permute-start.4
  66.0 3.4 %collective-permute-done.4 = f32[3,1,16,128]{3,0,2,1:T(4,128)S(1)} collective-permute-done((f32[3,1,16,128]{3,0,2,1:T(4,128)S(1)}, f32[3,1,16,128]{3,0,2,1:T(4,128)S(1)}, u32[]{:S(2)}, u32[]{:S(2)}) %collective-permute-start.4) | collective-permute-done | bytes 24608 | tf_op jit(solution)/shard_map/ppermute | solution.py:21
  69.4 1.6 collective-permute-start.7
  71.1 1.3 collective-permute-start.6
  72.7 4.2 %collective-permute-done.6 = f32[3,18,1,128]{3,0,2,1:T(4,128)S(1)} collective-permute-done((f32[3,18,1,128]{3,0,2,1:T(4,128)S(1)}, f32[3,18,1,128]{3,0,2,1:T(4,128)S(1)}, u32[]{:S(2)}, u32[]{:S(2)}) %collective-permute-start.6) | collective-permute-done | bytes 27680 | tf_op jit(solution)/shard_map/ppermute | solution.py:21
  77.0 0.8 select_maximum_fusion.4
  77.7 2.5 %multiply_reduce_fusion.2 = (f32[]{:T(128)}, f32[]{:T(128)}, f32[3,16,16,128]{3,0,2,1:T(4,128)S(1)}) fusion(f32[3,16,16,128]{3,0,2,1:T(4,128)S(1)} %convolution_add_fusion.1, f32[3,16,16,128]{3,2,1,0:T(8,128)S(1)} %copy-done.2, f32[3,18,18,130]{3,0,2,1:T(4,128)S(1)} %select_maximum_fusion.4, f32[16,16,128]{2,1,0:T(8,128)S(1)} %get-tuple-element.19, ...), kind=kOutput, calls=%fused_computation.86 | output fusion | flops 3178496 | bytes 3940360 | tf_op jit(solution)/shard_map/add | solution.py:53
  80.3 41.5 %all-reduce.6 = (f32[]{:T(128)}, f32[]{:T(128)}) all-reduce(f32[]{:T(128)} %get-tuple-element.7, f32[]{:T(128)} %get-tuple-element.6), channel_id=1, replica_groups=mesh['wide'=16,'narrow'=2] {'wide','narrow'}, use_global_device_ids=true, to_apply=%region_1.2 | all-reduce | flops 2 | bytes 16 | tf_op jit(solution)/shard_map/psum | solution.py:38
  123.1 1.7 convolution_bitcast_fusion
  125.0 39.1 %all-reduce.4 = f32[384]{0:T(512)S(1)} all-reduce(f32[384]{0:T(512)S(1)} %dynamic-update-slice.1), channel_id=1, replica_groups=mesh['wide'=16,'narrow'=2] {'wide','narrow'}, use_global_device_ids=true, to_apply=%add.4 | all-reduce | flops 384 | bytes 3072
  164.4 1.1 convolution_add_fusion
  165.5 1.3 collective-permute-start.9
  166.8 1.3 collective-permute-start.8
  168.1 4.3 %collective-permute-done.8 = f32[3,1,16,128]{3,0,2,1:T(4,128)S(1)} collective-permute-done((f32[3,1,16,128]{3,0,2,1:T(4,128)S(1)}, f32[3,1,16,128]{3,0,2,1:T(4,128)S(1)}, u32[]{:S(2)}, u32[]{:S(2)}) %collective-permute-start.8) | collective-permute-done | bytes 24608 | tf_op jit(solution)/shard_map/ppermute | solution.py:21
  172.4 3.3 %collective-permute-start.11 = (f32[3,18,1,128]{3,0,2,1:T(4,128)S(1)}, f32[3,18,1,128]{3,0,2,1:T(4,128)S(1)}, u32[]{:S(2)}, u32[]{:S(2)}) collective-permute-start(f32[3,18,1,128]{3,0,2,1:T(4,128)S(1)} %get-tuple-element.14), channel_id=1, source_target_pairs={{0,1},{2,3},{4,5},{6,7},{8,9},{10,11},{12,13},{14,15},{16,17},{18,... | collective-permute-start | bytes 82952 | tf_op jit(solution)/shard_map/ppermute | solution.py:20
  175.8 1.5 collective-permute-start.10
  177.4 4.2 %collective-permute-done.10 = f32[3,18,1,128]{3,0,2,1:T(4,128)S(1)} collective-permute-done((f32[3,18,1,128]{3,0,2,1:T(4,128)S(1)}, f32[3,18,1,128]{3,0,2,1:T(4,128)S(1)}, u32[]{:S(2)}, u32[]{:S(2)}) %collective-permute-start.10) | collective-permute-done | bytes 27680 | tf_op jit(solution)/shard_map/ppermute | solution.py:21
  181.6 0.8 select_maximum_fusion
  182.4 2.8 %multiply_reduce_fusion = (f32[]{:T(128)}, f32[]{:T(128)}, f32[3,16,16,128]{3,0,2,1:T(4,128)S(1)}) fusion(f32[3,16,16,128]{3,0,2,1:T(4,128)S(1)} %convolution_add_fusion, f32[3,16,16,128]{3,0,2,1:T(4,128)S(1)} %get-tuple-element.13, f32[]{:T(128)S(6)} %div.28, f32[3,16,16,128]{3,2,1,0:T(8,128)S(1)} %copy-done.2, ...), kind=kOutput, calls=%fused_computation.84 | output fusion | flops 3375104 | bytes 4464652 | tf_op jit(solution)/shard_map/add | solution.py:53
  185.2 41.7 %all-reduce.5 = (f32[]{:T(128)}, f32[]{:T(128)}) all-reduce(f32[]{:T(128)} %get-tuple-element.5, f32[]{:T(128)} %get-tuple-element.4), channel_id=1, replica_groups=mesh['wide'=16,'narrow'=2] {'wide','narrow'}, use_global_device_ids=true, to_apply=%region_6.7 | all-reduce | flops 2 | bytes 16 | tf_op jit(solution)/shard_map/psum | solution.py:38
  232.0 0.8 copy.15
  232.8 0.8 copy.14
  (37 shorter events, 2.6 us)
Async XLA Ops:
  0.6 57.0 %copy-start = (f32[12,384]{1,0:T(8,128)S(1)}, f32[12,384]{1,0:T(8,128)}, u32[]{:S(2)}) copy-start(f32[12,384]{1,0:T(8,128)} %param.7) | copy-start | bytes 55300
  0.6 61.6 %copy-start.1 = (s32[16,16,128]{2,1,0:T(8,128)S(1)}, s32[16,16,128]{2,1,0:T(8,128)}, u32[]{:S(2)}) copy-start(s32[16,16,128]{2,1,0:T(8,128)} %param.5) | copy-start | bytes 393220
  1.7 50.5 %collective-permute-start.1 = (f32[1,16,128]{2,1,0:T(8,128)S(1)}, f32[1,16,128]{2,1,0:T(8,128)S(1)}, u32[]{:S(2)}, u32[]{:S(2)}) collective-permute-start(f32[1,16,128]{2,1,0:T(8,128)S(1)} %get-tuple-element.32), channel_id=1, source_target_pairs={{0,2},{2,4},{4,6},{6,8},{8,10},{10,12},{12,14},{14,16},{16,18},{18... | collective-permute-start | bytes 24584 | tf_op jit(solution)/shard_map/ppermute | solution.py:20
  4.1 58.3 %copy-start.2 = (f32[3,16,16,128]{3,2,1,0:T(8,128)S(1)}, f32[3,16,16,128]{3,2,1,0:T(8,128)}, u32[]{:S(2)}) copy-start(f32[3,16,16,128]{3,2,1,0:T(8,128)} %param.4) | copy-start | bytes 1179652
  4.1 58.3 %copy-start.3 = (s32[16,16,128]{2,1,0:T(8,128)S(1)}, s32[16,16,128]{2,1,0:T(8,128)}, u32[]{:S(2)}) copy-start(s32[16,16,128]{2,1,0:T(8,128)} %param.6) | copy-start | bytes 393220
  4.1 48.1 %collective-permute-start = (f32[1,16,128]{2,1,0:T(8,128)S(1)}, f32[1,16,128]{2,1,0:T(8,128)S(1)}, u32[]{:S(2)}, u32[]{:S(2)}) collective-permute-start(f32[1,16,128]{2,1,0:T(8,128)S(1)} %get-tuple-element.33), channel_id=1, source_target_pairs={{2,0},{4,2},{6,4},{8,6},{10,8},{12,10},{14,12},{16,14},{18,16},{20... | collective-permute-start | bytes 24584 | tf_op jit(solution)/shard_map/ppermute | solution.py:21
  52.2 5.7 %collective-permute-start.3 = (f32[18,1,128]{2,1,0:T(1,128)S(1)}, f32[18,1,128]{2,1,0:T(1,128)S(1)}, u32[]{:S(2)}, u32[]{:S(2)}) collective-permute-start(f32[18,1,128]{2,1,0:T(1,128)S(1)} %get-tuple-element.27), channel_id=1, source_target_pairs={{0,1},{2,3},{4,5},{6,7},{8,9},{10,11},{12,13},{14,15},{16,17},{18,... | collective-permute-start | bytes 27656 | tf_op jit(solution)/shard_map/ppermute | solution.py:20
  56.4 5.6 %collective-permute-start.2 = (f32[18,1,128]{2,1,0:T(1,128)S(1)}, f32[18,1,128]{2,1,0:T(1,128)S(1)}, u32[]{:S(2)}, u32[]{:S(2)}) collective-permute-start(f32[18,1,128]{2,1,0:T(1,128)S(1)} %get-tuple-element.28), channel_id=1, source_target_pairs={{1,0},{3,2},{5,4},{7,6},{9,8},{11,10},{13,12},{15,14},{17,16},{19,... | collective-permute-start | bytes 27656 | tf_op jit(solution)/shard_map/ppermute | solution.py:21
  63.4 2.6 %collective-permute-start.5 = (f32[3,1,16,128]{3,0,2,1:T(4,128)S(1)}, f32[3,1,16,128]{3,0,2,1:T(4,128)S(1)}, u32[]{:S(2)}, u32[]{:S(2)}) collective-permute-start(f32[3,1,16,128]{3,0,2,1:T(4,128)S(1)} %get-tuple-element.22), channel_id=1, source_target_pairs={{0,2},{2,4},{4,6},{6,8},{8,10},{10,12},{12,14},{14,16},{16,18},{18... | collective-permute-start | bytes 73736 | tf_op jit(solution)/shard_map/ppermute | solution.py:20
  64.7 4.7 %collective-permute-start.4 = (f32[3,1,16,128]{3,0,2,1:T(4,128)S(1)}, f32[3,1,16,128]{3,0,2,1:T(4,128)S(1)}, u32[]{:S(2)}, u32[]{:S(2)}) collective-permute-start(f32[3,1,16,128]{3,0,2,1:T(4,128)S(1)} %get-tuple-element.23), channel_id=1, source_target_pairs={{2,0},{4,2},{6,4},{8,6},{10,8},{12,10},{14,12},{16,14},{18,16},{20... | collective-permute-start | bytes 73736 | tf_op jit(solution)/shard_map/ppermute | solution.py:21
  69.4 3.3 %collective-permute-start.7 = (f32[3,18,1,128]{3,0,2,1:T(4,128)S(1)}, f32[3,18,1,128]{3,0,2,1:T(4,128)S(1)}, u32[]{:S(2)}, u32[]{:S(2)}) collective-permute-start(f32[3,18,1,128]{3,0,2,1:T(4,128)S(1)} %get-tuple-element.16), channel_id=1, source_target_pairs={{0,1},{2,3},{4,5},{6,7},{8,9},{10,11},{12,13},{14,15},{16,17},{18,... | collective-permute-start | bytes 82952 | tf_op jit(solution)/shard_map/ppermute | solution.py:20
  71.1 5.9 %collective-permute-start.6 = (f32[3,18,1,128]{3,0,2,1:T(4,128)S(1)}, f32[3,18,1,128]{3,0,2,1:T(4,128)S(1)}, u32[]{:S(2)}, u32[]{:S(2)}) collective-permute-start(f32[3,18,1,128]{3,0,2,1:T(4,128)S(1)} %get-tuple-element.17), channel_id=1, source_target_pairs={{1,0},{3,2},{5,4},{7,6},{9,8},{11,10},{13,12},{15,14},{17,16},{19,... | collective-permute-start | bytes 82952 | tf_op jit(solution)/shard_map/ppermute | solution.py:21
  165.5 2.6 %collective-permute-start.9 = (f32[3,1,16,128]{3,0,2,1:T(4,128)S(1)}, f32[3,1,16,128]{3,0,2,1:T(4,128)S(1)}, u32[]{:S(2)}, u32[]{:S(2)}) collective-permute-start(f32[3,1,16,128]{3,0,2,1:T(4,128)S(1)} %get-tuple-element.20), channel_id=1, source_target_pairs={{0,2},{2,4},{4,6},{6,8},{8,10},{10,12},{12,14},{14,16},{16,18},{18... | collective-permute-start | bytes 73736 | tf_op jit(solution)/shard_map/ppermute | solution.py:20
  166.8 5.6 %collective-permute-start.8 = (f32[3,1,16,128]{3,0,2,1:T(4,128)S(1)}, f32[3,1,16,128]{3,0,2,1:T(4,128)S(1)}, u32[]{:S(2)}, u32[]{:S(2)}) collective-permute-start(f32[3,1,16,128]{3,0,2,1:T(4,128)S(1)} %get-tuple-element.21), channel_id=1, source_target_pairs={{2,0},{4,2},{6,4},{8,6},{10,8},{12,10},{14,12},{16,14},{18,16},{20... | collective-permute-start | bytes 73736 | tf_op jit(solution)/shard_map/ppermute | solution.py:21
  172.4 4.9 %collective-permute-start.11 = (f32[3,18,1,128]{3,0,2,1:T(4,128)S(1)}, f32[3,18,1,128]{3,0,2,1:T(4,128)S(1)}, u32[]{:S(2)}, u32[]{:S(2)}) collective-permute-start(f32[3,18,1,128]{3,0,2,1:T(4,128)S(1)} %get-tuple-element.14), channel_id=1, source_target_pairs={{0,1},{2,3},{4,5},{6,7},{8,9},{10,11},{12,13},{14,15},{16,17},{18,... | collective-permute-start | bytes 82952 | tf_op jit(solution)/shard_map/ppermute | solution.py:20
  175.8 5.9 %collective-permute-start.10 = (f32[3,18,1,128]{3,0,2,1:T(4,128)S(1)}, f32[3,18,1,128]{3,0,2,1:T(4,128)S(1)}, u32[]{:S(2)}, u32[]{:S(2)}) collective-permute-start(f32[3,18,1,128]{3,0,2,1:T(4,128)S(1)} %get-tuple-element.15), channel_id=1, source_target_pairs={{1,0},{3,2},{5,4},{7,6},{9,8},{11,10},{13,12},{15,14},{17,16},{19,... | collective-permute-start | bytes 82952 | tf_op jit(solution)/shard_map/ppermute | solution.py:21
where the time goes:
time: 235 us; the launch traced here: 234 us
  blocking collectives  166 us (71%)
  starting transfers between devices  22.2 us (9%)
  waiting for transfers between devices  20.6 us (9%)
  other arithmetic  8.98 us (4%)
  between operations  6.82 us (3%)
  matrix products  6.49 us (3%)
  local copies, waits for them, and re-layouts  2.36 us (1%)
    psum x2, blocking collectives, paired_sums(): lax.psum((jnp.sum(resid * precond), jnp.sum(image * precond)), ('wide', '...  83.2 us
    unnamed x2, blocking collectives  83 us
    ppermute x6, waiting for transfers between devices, padded_2(): after = lax.ppermute(first, axis, down)  20.2 us
    ppermute x6, starting transfers between devices, padded_2(): before = lax.ppermute(last, axis, up)  14.1 us
    ppermute x6, starting transfers between devices, padded_2(): after = lax.ppermute(first, axis, down)  8.06 us
    add x2, other arithmetic, operate(): result = 0.25 * stiff * (field + jnp.sum(field, axis=0, keepdims=True))  5.33 us
  transfers between devices with their start and end apart: 12, of which 7 were waited for; matrix products, arithmetic and copies ran while one was open for 1% of the time, Pallas kernels for 0%

commit v1 on v0

v1 whole, which is shorter than its diff:
```python
import functools

import jax
import jax.numpy as jnp
from jax import lax
from jax.experimental import pallas as pl
from jax.experimental.pallas import tpu as pltpu
from jax.sharding import PartitionSpec as P

LANES = 128
SUB = 8
MESH = pl.DeviceIdType.MESH
bone_stiff = 1.0
soft_stiff = 0.1


def kernel(nw, nn, r_hbm, occ_hbm, reg_hbm, ci_hbm, x_out, res_out,
           r_v, occ_v, reg_v, c_v, k_p, kx, kym, kyp, kzm, kzp, dg, invd,
           z_p, y_v, v_p, az_v, zy, vy,
           ix_in, iy_send, iy_in, c_in, wx_send, wx_in, wy_send, wy_in,
           row_send, rows, load_sem, hs_send, hs_recv, ag_send, ag_recv):
    X, Y, Z = occ_v.shape
    ncr, NC = c_v.shape
    G = ncr // 3
    ND = nw * nn
    wi = lax.axis_index("wide")
    ni = lax.axis_index("narrow")
    me = wi * nn + ni
    f32 = jnp.float32

    loads = [pltpu.make_async_copy(s, d, load_sem.at[i]) for i, (s, d) in enumerate(
        ((occ_hbm, occ_v), (reg_hbm, reg_v), (r_hbm, r_v), (ci_hbm, c_v)))]
    for l in loads:
        l.start()

    def peer(i):
        t = lax.rem(me + i, ND)
        return (t // nn, lax.rem(t, nn))

    barrier = pltpu.get_barrier_semaphore()

    def greet(i, _):
        pl.semaphore_signal(barrier, inc=1, device_id=peer(i), device_id_type=MESH)
        return 0

    lax.fori_loop(1, ND, greet, 0, unroll=ND <= 64)

    has = (wi > 0, wi < nw - 1, ni > 0, ni < nn - 1)
    to = ((wi - 1, ni), (wi + 1, ni), (wi, ni - 1), (wi, ni + 1))

    for d in range(4):
        @pl.when(jnp.logical_not(has[d]))
        def _():
            c_in[d] = jnp.zeros((ncr, NC), f32)
            for p in range(2):
                if d < 2:
                    wx_in[p, d] = jnp.zeros((3, Y, Z), f32)
                else:
                    wy_in[p, d - 2] = jnp.zeros((3, X, Z), f32)
            if d < 2:
                ix_in[d] = jnp.zeros((2, Y, Z), jnp.int32)
            else:
                iy_in[d - 2] = jnp.zeros((2, X, Z), jnp.int32)

    loads[0].wait()
    loads[1].wait()

    def pack_ints(x, _):
        iy_send[0, 0, pl.ds(x, 1), :] = occ_v[x, 0:1, :]
        iy_send[1, 0, pl.ds(x, 1), :] = occ_v[x, Y - 1:Y, :]
        iy_send[0, 1, pl.ds(x, 1), :] = reg_v[x, 0:1, :]
        iy_send[1, 1, pl.ds(x, 1), :] = reg_v[x, Y - 1:Y, :]
        return 0

    lax.fori_loop(0, X, pack_ints, 0)

    def fold(a):
        return jnp.sum(a.reshape(Y // SUB, SUB, Z), axis=0)

    def zero_acc(n):
        return tuple(jnp.zeros((SUB, Z), f32) for _ in range(n))

    def add_rc(acc, reg, u):
        out = list(acc)
        for g in range(G):
            m = reg == g
            for c in range(3):
                out[g * 3 + c] = acc[g * 3 + c] + fold(jnp.where(m, u[c], 0.0))
        return tuple(out)

    base = (me * ncr) % LANES

    def make_row(p, acc, first):
        a = jnp.concatenate([jnp.sum(b, axis=0, keepdims=True) for b in acc], axis=0)
        col = jnp.sum(a, axis=1, keepdims=True)
        n = len(acc)
        k = lax.broadcasted_iota(jnp.int32, (n, LANES), 0)
        lane = lax.broadcasted_iota(jnp.int32, (n, LANES), 1)
        target = (base + first + k) & (LANES - 1)
        row = jnp.sum(jnp.where(lane == target, col, 0.0), axis=0, keepdims=True)
        row_send[p, 0:1, :] = row
        rows[p, pl.ds(me, 1), :] = row

    def gather_start(p):
        def send(i, _):
            pltpu.make_async_remote_copy(
                src_ref=row_send.at[p, pl.ds(0, 1)], dst_ref=rows.at[p, pl.ds(me, 1)],
                send_sem=ag_send.at[p], recv_sem=ag_recv.at[p],
                device_id=peer(i), device_id_type=MESH).start()
            return 0
        lax.fori_loop(1, ND, send, 0, unroll=ND <= 64)

    def gather_wait(p, sem):
        part = rows.at[p, pl.ds(0, ND - 1)]
        pltpu.make_async_copy(part, part, sem.at[p]).wait()

    def coarse_vector(p):
        tiles = []
        for t in range(NC // LANES):
            lo = (LANES * t) // ncr // SUB * SUB
            hi = min(ND, -(-(-(-(LANES * (t + 1)) // ncr)) // SUB) * SUB)
            d = lax.broadcasted_iota(jnp.int32, (hi - lo, LANES), 0) + lo
            j = lax.broadcasted_iota(jnp.int32, (hi - lo, LANES), 1) + LANES * t
            m = (j >= d * ncr) & (j < d * ncr + ncr)
            tiles.append(jnp.sum(jnp.where(m, rows[p, lo:hi, :], 0.0), axis=0, keepdims=True))
        return tiles

    def total(p, s):
        d = lax.broadcasted_iota(jnp.int32, (ND, LANES), 0)
        lane = lax.broadcasted_iota(jnp.int32, (ND, LANES), 1)
        m = lane == ((d * ncr + ncr + s) & (LANES - 1))
        v = jnp.sum(jnp.where(m, rows[p], 0.0), axis=0, keepdims=True)
        return jnp.sum(v, axis=1, keepdims=True)

    def answers(tiles, ref):
        s = ref[:, 0:LANES] * tiles[0]
        for t in range(1, len(tiles)):
            s = s + ref[:, t * LANES:(t + 1) * LANES] * tiles[t]
        q = jnp.sum(s, axis=1, keepdims=True)
        return [q[i:i + 1, :] for i in range(ncr)]

    def spread(reg, q):
        masks = [reg == g for g in range(G)]
        out = []
        for c in range(3):
            s = jnp.zeros(reg.shape, f32)
            for g in range(G):
                s = jnp.where(masks[g], q[g * 3 + c], s)
            out.append(s)
        return out

    def halo(slot, d, src, dst):
        return pltpu.make_async_remote_copy(
            src_ref=src, dst_ref=dst, send_sem=hs_send.at[slot, d],
            recv_sem=hs_recv.at[slot, d ^ 1], device_id=to[d], device_id_type=MESH)

    def copies(kind, d):
        e = d ^ 1
        if kind == 0:
            if d < 2:
                x = 0 if d == 0 else X - 1
                return [halo(0, d, occ_v.at[x], ix_in.at[e, 0]),
                        halo(1, d, reg_v.at[x], ix_in.at[e, 1])]
            return [halo(0, d, iy_send.at[d - 2, 0], iy_in.at[e - 2, 0]),
                    halo(1, d, iy_send.at[d - 2, 1], iy_in.at[e - 2, 1])]
        if kind == 1:
            return [halo(2, d, c_v, c_in.at[e])]
        p = kind - 2
        if d < 2:
            return [halo(3 + p, d, wx_send.at[p, d], wx_in.at[p, e])]
        return [halo(3 + p, d, wy_send.at[p, d - 2], wy_in.at[p, e - 2])]

    def halo_start(kind):
        for d in range(4):
            @pl.when(has[d])
            def _():
                for c in copies(kind, d):
                    c.start()

    def halo_wait(kind):
        for d in range(4):
            @pl.when(has[d])
            def _():
                for c in copies(kind, d ^ 1):
                    c.wait_recv()

    def halo_done(kind):
        for d in range(4):
            @pl.when(has[d])
            def _():
                for c in copies(kind, d):
                    c.wait_send()

    loads[2].wait()
    acc = lax.fori_loop(0, X, lambda x, a: add_rc(a, reg_v[x], [r_v[c, x] for c in range(3)]),
                        zero_acc(ncr))
    make_row(0, acc, 0)
    loads[3].wait()

    pl.semaphore_wait(barrier, ND - 1)
    halo_start(0)
    gather_start(0)
    halo_start(1)

    def stiff_of(o):
        return soft_stiff + (bone_stiff - soft_stiff) * o.astype(f32)

    def own_k(x, _):
        k_p[x + 1] = stiff_of(occ_v[x])
        return 0

    lax.fori_loop(0, X, own_k, 0)
    halo_wait(0)
    for d in range(2):
        @pl.when(has[d])
        def _():
            k_p[0 if d == 0 else X + 1] = stiff_of(ix_in[d, 0])

        @pl.when(jnp.logical_not(has[d]))
        def _():
            k_p[0 if d == 0 else X + 1] = jnp.zeros((Y, Z), f32)

    row_id = lax.broadcasted_iota(jnp.int32, (Y, Z), 0)
    lane_id = lax.broadcasted_iota(jnp.int32, (Y, Z), 1)
    side_lo = jnp.where(has[2], 1.0, 0.0).astype(f32)
    side_hi = jnp.where(has[3], 1.0, 0.0).astype(f32)

    def yshift(u, lo, hi):
        down = jnp.where(row_id == 0, lo, pltpu.roll(u, 1, 0))
        up = jnp.where(row_id == Y - 1, hi, pltpu.roll(u, Y - 1, 0))
        return down, up

    def save_faces(p, x, w):
        for c in range(3):
            wy_send[p, 0, c, pl.ds(x, 1), :] = w[c][0:1, :]
            wy_send[p, 1, c, pl.ds(x, 1), :] = w[c][Y - 1:Y, :]

    def coefficients(x, _):
        k = k_p[x + 1]
        lo = stiff_of(iy_in[0, 0, pl.ds(x, 1), :]) * side_lo
        hi = stiff_of(iy_in[1, 0, pl.ds(x, 1), :]) * side_hi
        down, up = yshift(k, lo, hi)
        back = jnp.where(lane_id == 0, 0.0, pltpu.roll(k, 1, 1))
        ahead = jnp.where(lane_id == Z - 1, 0.0, pltpu.roll(k, Z - 1, 1))
        xm = 0.5 * (k + k_p[x])
        xp = 0.5 * (k + k_p[x + 2])
        ym = 0.5 * (k + down)
        yp = 0.5 * (k + up)
        zm = 0.5 * (k + back)
        zp = 0.5 * (k + ahead)
        diag = xm + xp + ym + yp + zm + zp + 0.5 * k
        inv = 1.0 / diag
        kx[x] = xm
        kx[x + 1] = xp
        kym[x] = ym
        kyp[x] = yp
        kzm[x] = jnp.where(lane_id == 0, 0.0, zm)
        kzp[x] = jnp.where(lane_id == Z - 1, 0.0, zp)
        dg[x] = diag - 0.25 * k
        invd[x] = inv
        w = [r_v[c, x] * inv for c in range(3)]
        for c in range(3):
            z_p[c, x + 1] = w[c]
        save_faces(0, x, w)
        return 0

    lax.fori_loop(0, X, coefficients, 0)
    for c in range(3):
        wx_send[0, 0, c] = z_p[c, 1]
        wx_send[0, 1, c] = z_p[c, X]
    halo_start(2)

    def edges(p, qs, pad, side):
        for d in range(2):
            s = spread(ix_in[d, 1], qs[d])
            for c in range(3):
                pad[c, 0 if d == 0 else X + 1] = wx_in[p, d, c] + s[c]
        for d in range(2):
            s = spread(iy_in[d, 1], qs[2 + d])
            for c in range(3):
                side[d, c] = wy_in[p, d, c] + s[c]

    def operate(pad, side, x):
        k = k_p[x + 1]
        u = [pad[c, x + 1] for c in range(3)]
        k4 = 0.25 * k * (u[0] + u[1] + u[2])
        out = []
        for c in range(3):
            down, up = yshift(u[c], side[0, c, pl.ds(x, 1), :], side[1, c, pl.ds(x, 1), :])
            a = dg[x] * u[c] + k4
            a = a - (kx[x] * pad[c, x] + kx[x + 1] * pad[c, x + 2])
            a = a - (kym[x] * down + kyp[x] * up)
            a = a - (kzm[x] * pltpu.roll(u[c], 1, 1) + kzp[x] * pltpu.roll(u[c], Z - 1, 1))
            out.append(a)
        return u, out

    gather_wait(0, ag_recv)
    halo_wait(1)
    tiles = coarse_vector(0)
    q = answers(tiles, c_v)
    qs = [answers(tiles, c_in.at[d]) for d in range(4)]

    def add_spread(x, _):
        s = spread(reg_v[x], q)
        for c in range(3):
            z_p[c, x + 1] = z_p[c, x + 1] + s[c]
        return 0

    lax.fori_loop(0, X, add_spread, 0)
    halo_wait(2)
    edges(0, qs, z_p, zy)

    def dots(a, b):
        return fold(a[0] * b[0] + a[1] * b[1] + a[2] * b[2])

    def first(x, carry):
        u, a = operate(z_p, zy, x)
        r = [r_v[c, x] for c in range(3)]
        w = []
        for c in range(3):
            y_v[c, x] = a[c]
            w.append(a[c] * invd[x])
            v_p[c, x + 1] = w[c]
        save_faces(1, x, w)
        acc = add_rc(carry[:ncr], reg_v[x], a)
        return acc + (carry[ncr] + dots(r, u), carry[ncr + 1] + dots(a, u))

    acc = lax.fori_loop(0, X, first, zero_acc(ncr + 2))
    make_row(1, acc, 0)
    gather_start(1)
    for c in range(3):
        wx_send[1, 0, c] = v_p[c, 1]
        wx_send[1, 1, c] = v_p[c, X]
    halo_start(3)
    halo_wait(3)
    gather_wait(1, ag_recv)
    tiles = coarse_vector(1)
    q = answers(tiles, c_v)
    qs = [answers(tiles, c_in.at[d]) for d in range(4)]
    rz0 = total(1, 0)
    alpha0 = rz0 / total(1, 1)

    def add_spread_v(x, _):
        s = spread(reg_v[x], q)
        for c in range(3):
            v_p[c, x + 1] = v_p[c, x + 1] + s[c]
        return 0

    lax.fori_loop(0, X, add_spread_v, 0)
    edges(1, qs, v_p, vy)

    def second(x, carry):
        u, a = operate(v_p, vy, x)
        r, z, az = [], [], []
        for c in range(3):
            y = y_v[c, x]
            r.append(r_v[c, x] - alpha0 * y)
            z.append(z_p[c, x + 1] - alpha0 * u[c])
            az.append(y - alpha0 * a[c])
            r_v[c, x] = r[c]
            x_out[c, x] = z[c]
            az_v[c, x] = az[c]
        return (carry[0] + dots(r, z), carry[1] + dots(az, z))

    acc = lax.fori_loop(0, X, second, zero_acc(2))
    make_row(2, acc, ncr)
    gather_start(2)
    gather_wait(2, ag_recv)
    rz1 = total(2, 0)
    beta = rz1 / rz0
    alpha1 = rz1 / (total(2, 1) - beta * rz1 / alpha0)
    along = alpha0 + alpha1 * beta
    a1b = alpha1 * beta

    def last(x, _):
        for c in range(3):
            x_out[c, x] = along * z_p[c, x + 1] + alpha1 * x_out[c, x]
            res_out[c, x] = r_v[c, x] - alpha1 * az_v[c, x] - a1b * y_v[c, x]
        return 0

    lax.fori_loop(0, X, last, 0)
    for kind in range(4):
        halo_done(kind)
    for p in range(3):
        gather_wait(p, ag_send)


def local(nw, nn, right_side, occupancy, region, coarse_inverse):
    _, X, Y, Z = right_side.shape
    ncr, NC = coarse_inverse.shape
    ND = nw * nn
    f32, i32 = jnp.float32, jnp.int32
    V = pltpu.VMEM
    field, pad, scal = (3, X, Y, Z), (3, X + 2, Y, Z), (X, Y, Z)
    scratch = [
        V(field, f32), V(scal, i32), V(scal, i32), V((ncr, NC), f32),
        V((X + 2, Y, Z), f32), V((X + 1, Y, Z), f32),
        V(scal, f32), V(scal, f32), V(scal, f32), V(scal, f32), V(scal, f32), V(scal, f32),
        V(pad, f32), V(field, f32), V(pad, f32), V(field, f32),
        V((2, 3, X, Z), f32), V((2, 3, X, Z), f32),
        V((2, 2, Y, Z), i32), V((2, 2, X, Z), i32), V((2, 2, X, Z), i32),
        V((4, ncr, NC), f32),
        V((2, 2, 3, Y, Z), f32), V((2, 2, 3, Y, Z), f32),
        V((2, 2, 3, X, Z), f32), V((2, 2, 3, X, Z), f32),
        V((3, SUB, LANES), f32), V((3, ND, LANES), f32),
        pltpu.SemaphoreType.DMA((4,)),
        pltpu.SemaphoreType.DMA((5, 4)), pltpu.SemaphoreType.DMA((5, 4)),
        pltpu.SemaphoreType.DMA((3,)), pltpu.SemaphoreType.DMA((3,)),
    ]
    return pl.pallas_call(
        functools.partial(kernel, nw, nn),
        out_shape=(jax.ShapeDtypeStruct(field, f32), jax.ShapeDtypeStruct(field, f32)),
        in_specs=[pl.BlockSpec(memory_space=pl.ANY)] * 4,
        out_specs=(pl.BlockSpec(memory_space=pltpu.VMEM),) * 2,
        scratch_shapes=scratch,
        compiler_params=pltpu.CompilerParams(collective_id=0, has_side_effects=True),
    )(right_side, occupancy, region, coarse_inverse)


def solution(mesh):
    return jax.shard_map(
        functools.partial(local, mesh.shape["wide"], mesh.shape["narrow"]),
        mesh=mesh,
        in_specs=(
            P(None, "wide", "narrow", None),
            P("wide", "narrow", None),
            P("wide", "narrow", None),
            P(("wide", "narrow"), None),
        ),
        out_specs=(P(None, "wide", "narrow", None), P(None, "wide", "narrow", None)),
        check_vma=False,
    )
```

time: 235 us -> 31.3 us (0.13)
  blocking collectives: 166 us -> 0 us
  Pallas kernels: 0 us -> 27.9 us
  starting transfers between devices: 22.2 us -> 0 us
  waiting for transfers between devices: 20.6 us -> 0 us
  other arithmetic: 8.98 us -> 0 us
  matrix products: 6.49 us -> 0 us
  between operations: 6.82 us -> 0.65 us
    psum x2 -> x0, blocking collectives: 83.2 us -> none  [paired_sums(): lax.psum((jnp.sum(resid * precond), jnp.sum(image * precond)), ('wide', '...]
    unnamed x2 -> x0, blocking collectives: 83 us -> none
    pallas_call x0 -> x1, Pallas kernels: none -> 27.9 us  [local(): pl.pallas_call(functools.partial(kernel, nw, nn), out_shape=(jax.ShapeDty...]
    ppermute x12 -> x0, starting transfers between devices: 22.2 us -> none  [the longest x6 14.1 us: padded_2(): before = lax.ppermute(last, axis, up)]
    ppermute x12 -> x0, waiting for transfers between devices: 20.6 us -> none  [the longest x6 20.2 us: padded_2(): after = lax.ppermute(first, axis, down)]
    dot_general x6 -> x0, matrix products: 6.49 us -> none  [the longest x2 4.19 us: precondition(): jnp.einsum('gxyz,cxyz->gc', onehot, resid, precision=lax.Precision.HIGHEST)]
    add x3 -> x0, other arithmetic: 6.31 us -> none  [the longest x2 5.33 us: operate(): result = 0.25 * stiff * (field + jnp.sum(field, axis=0, keepdims=True))]
  transfers between devices with their start and end apart: 12 -> 0, of which waited for: 7 -> 0; matrix products, arithmetic and copies ran while one was open for 1% -> 0% of each run, Pallas kernels for 0% -> 0%
where the time goes in v1:
time: 31.3 us; the launch traced here: 31.1 us
  Pallas kernels  27.9 us (89%)
  local copies, waits for them, and re-layouts  2.57 us (8%)
  between operations  0.65 us (2%)
    pallas_call x1, Pallas kernels, local(): pl.pallas_call(functools.partial(kernel, nw, nn), out_shape=(jax.ShapeDty...  27.9 us
    unnamed x4, local copies, waits for them, and re-layouts  2.57 us

profile of v1, /device:TPU:0, one launch (start us, length us, event | category | flops | bytes accessed | tf_op | source)
XLA Modules:
  0.0 31.1 jit_solution(1464967108069138182)
XLA Ops:
  0.6 27.9 %shard_map.59 = (f32[3,16,16,128]{3,2,1,0:T(8,128)}, f32[3,16,16,128]{3,2,1,0:T(8,128)}) custom-call(f32[3,16,16,128]{3,2,1,0:T(8,128)} %r_hbm.1, s32[16,16,128]{2,1,0:T(8,128)} %occ_hbm.1, s32[16,16,128]{2,1,0:T(8,128)} %reg_hbm.1, f32[12,384]{1,0:T(8,128)} %ci_hbm.1), custom_call_target="tpu_custom_call" | custom-call | tf_op jit(solution)/shard_map/pallas_call | solution.py:410
  28.6 0.0 copy-start
  28.6 1.8 %copy.8 = f32[3,16,16,128]{3,2,1,0:T(8,128)} copy(f32[3,16,16,128]{3,2,1,0:T(8,128)} %get-tuple-element.4) | data formatting | bytes 786432
  30.4 0.0 copy-done
  30.4 0.7 %copy.9 = f32[3,16,16,128]{3,2,1,0:T(8,128)} copy(f32[3,16,16,128]{3,2,1,0:T(8,128)S(1)} %copy-done) | data formatting | bytes 786432
Async XLA Ops:
  28.6 1.8 %copy-start = (f32[3,16,16,128]{3,2,1,0:T(8,128)S(1)}, f32[3,16,16,128]{3,2,1,0:T(8,128)}, u32[]{:S(2)}) copy-start(f32[3,16,16,128]{3,2,1,0:T(8,128)} %get-tuple-element.5) | copy-start | bytes 1179652

commit v2 on v1

--- a/solution.py
+++ b/solution.py
@@ -9,14 +9,17 @@
 
 LANES = 128
 SUB = 8
+UNROLL = 16
+looped = functools.partial(lax.fori_loop, unroll=UNROLL)
 MESH = pl.DeviceIdType.MESH
 bone_stiff = 1.0
 soft_stiff = 0.1
 
 
-def kernel(nw, nn, r_hbm, occ_hbm, reg_hbm, ci_hbm, x_out, res_out,
-           r_v, occ_v, reg_v, c_v, k_p, kx, kym, kyp, kzm, kzp, dg, invd,
-           z_p, y_v, v_p, az_v, zy, vy,
+def kernel(nw, nn, r_hbm, occ_hbm, reg_hbm, ci_hbm,
+           z0_v, z1_v, r_v, az_v, y_v, sc_v,
+            occ_v, reg_v, c_v, k_p, kx, kym, kyp, kzm, kzp, dg, invd,
+           z_p, v_p, zy, vy,
            ix_in, iy_send, iy_in, c_in, wx_send, wx_in, wy_send, wy_in,
            row_send, rows, load_sem, hs_send, hs_recv, ag_send, ag_recv):
     X, Y, Z = occ_v.shape
@@ -72,7 +75,7 @@
         iy_send[1, 1, pl.ds(x, 1), :] = reg_v[x, Y - 1:Y, :]
         return 0
 
-    lax.fori_loop(0, X, pack_ints, 0)
+    looped(0, X, pack_ints, 0)
 
     def fold(a):
         return jnp.sum(a.reshape(Y // SUB, SUB, Z), axis=0)
@@ -192,7 +195,7 @@
                     c.wait_send()
 
     loads[2].wait()
-    acc = lax.fori_loop(0, X, lambda x, a: add_rc(a, reg_v[x], [r_v[c, x] for c in range(3)]),
+    acc = looped(0, X, lambda x, a: add_rc(a, reg_v[x], [r_v[c, x] for c in range(3)]),
                         zero_acc(ncr))
     make_row(0, acc, 0)
     loads[3].wait()
@@ -209,7 +212,7 @@
         k_p[x + 1] = stiff_of(occ_v[x])
         return 0
 
-    lax.fori_loop(0, X, own_k, 0)
+    looped(0, X, own_k, 0)
     halo_wait(0)
     for d in range(2):
         @pl.when(has[d])
@@ -264,7 +267,7 @@
         save_faces(0, x, w)
         return 0
 
-    lax.fori_loop(0, X, coefficients, 0)
+    looped(0, X, coefficients, 0)
     for c in range(3):
         wx_send[0, 0, c] = z_p[c, 1]
         wx_send[0, 1, c] = z_p[c, X]
@@ -303,10 +306,12 @@
     def add_spread(x, _):
         s = spread(reg_v[x], q)
         for c in range(3):
-            z_p[c, x + 1] = z_p[c, x + 1] + s[c]
-        return 0
-
-    lax.fori_loop(0, X, add_spread, 0)
+            z = z_p[c, x + 1] + s[c]
+            z_p[c, x + 1] = z
+            z0_v[c, x] = z
+        return 0
+
+    looped(0, X, add_spread, 0)
     halo_wait(2)
     edges(0, qs, z_p, zy)
 
@@ -325,7 +330,7 @@
         acc = add_rc(carry[:ncr], reg_v[x], a)
         return acc + (carry[ncr] + dots(r, u), carry[ncr + 1] + dots(a, u))
 
-    acc = lax.fori_loop(0, X, first, zero_acc(ncr + 2))
+    acc = looped(0, X, first, zero_acc(ncr + 2))
     make_row(1, acc, 0)
     gather_start(1)
     for c in range(3):
@@ -346,7 +351,7 @@
             v_p[c, x + 1] = v_p[c, x + 1] + s[c]
         return 0
 
-    lax.fori_loop(0, X, add_spread_v, 0)
+    looped(0, X, add_spread_v, 0)
     edges(1, qs, v_p, vy)
 
     def second(x, carry):
@@ -358,11 +363,11 @@
             z.append(z_p[c, x + 1] - alpha0 * u[c])
             az.append(y - alpha0 * a[c])
             r_v[c, x] = r[c]
-            x_out[c, x] = z[c]
+            z1_v[c, x] = z[c]
             az_v[c, x] = az[c]
         return (carry[0] + dots(r, z), carry[1] + dots(az, z))
 
-    acc = lax.fori_loop(0, X, second, zero_acc(2))
+    acc = looped(0, X, second, zero_acc(2))
     make_row(2, acc, ncr)
     gather_start(2)
     gather_wait(2, ag_recv)
@@ -372,17 +377,23 @@
     along = alpha0 + alpha1 * beta
     a1b = alpha1 * beta
 
-    def last(x, _):
-        for c in range(3):
-            x_out[c, x] = along * z_p[c, x + 1] + alpha1 * x_out[c, x]
-            res_out[c, x] = r_v[c, x] - alpha1 * az_v[c, x] - a1b * y_v[c, x]
-        return 0
-
-    lax.fori_loop(0, X, last, 0)
+    sc_v[0:1, :] = jnp.broadcast_to(along, (1, LANES))
+    sc_v[1:2, :] = jnp.broadcast_to(alpha1, (1, LANES))
+    sc_v[2:3, :] = jnp.broadcast_to(a1b, (1, LANES))
     for kind in range(4):
         halo_done(kind)
     for p in range(3):
         gather_wait(p, ag_send)
+
+
+def finish(z0_v, z1_v, r_v, az_v, y_v, sc_v, x_out, res_out):
+    c = pl.program_id(0)
+    along = sc_v[0:1, 0:1]
+    alpha1 = sc_v[1:2, 0:1]
+    a1b = sc_v[2:3, 0:1]
+    for x in range(x_out.shape[1]):
+        x_out[0, x] = along * z0_v[c, x] + alpha1 * z1_v[c, x]
+        res_out[0, x] = r_v[c, x] - alpha1 * az_v[c, x] - a1b * y_v[c, x]
 
 
 def local(nw, nn, right_side, occupancy, region, coarse_inverse):
@@ -393,10 +404,10 @@
     V = pltpu.VMEM
     field, pad, scal = (3, X, Y, Z), (3, X + 2, Y, Z), (X, Y, Z)
     scratch = [
-        V(field, f32), V(scal, i32), V(scal, i32), V((ncr, NC), f32),
+        V(scal, i32), V(scal, i32), V((ncr, NC), f32),
         V((X + 2, Y, Z), f32), V((X + 1, Y, Z), f32),
         V(scal, f32), V(scal, f32), V(scal, f32), V(scal, f32), V(scal, f32), V(scal, f32),
-        V(pad, f32), V(field, f32), V(pad, f32), V(field, f32),
+        V(pad, f32), V(pad, f32),
         V((2, 3, X, Z), f32), V((2, 3, X, Z), f32),
         V((2, 2, Y, Z), i32), V((2, 2, X, Z), i32), V((2, 2, X, Z), i32),
         V((4, ncr, NC), f32),
@@ -407,14 +418,23 @@
         pltpu.SemaphoreType.DMA((5, 4)), pltpu.SemaphoreType.DMA((5, 4)),
         pltpu.SemaphoreType.DMA((3,)), pltpu.SemaphoreType.DMA((3,)),
     ]
+    parts = pl.pallas_call(
+        functools.partial(kernel, nw, nn),
+        out_shape=(V(field, f32),) * 5 + (V((SUB, LANES), f32),),
+        in_specs=[pl.BlockSpec(memory_space=pltpu.HBM)] * 4,
+        out_specs=(pl.BlockSpec(memory_space=pltpu.VMEM),) * 6,
+        scratch_shapes=scratch,
+        compiler_params=pltpu.CompilerParams(collective_id=0, has_side_effects=True, vmem_limit_bytes=32 * 1024 * 1024),
+    )(*[pltpu.with_memory_space_constraint(a, pltpu.HBM) for a in (right_side, occupancy, region, coarse_inverse)])
+    block = pl.BlockSpec((1, X, Y, Z), lambda c: (c, 0, 0, 0))
     return pl.pallas_call(
-        functools.partial(kernel, nw, nn),
-        out_shape=(jax.ShapeDtypeStruct(field, f32), jax.ShapeDtypeStruct(field, f32)),
-        in_specs=[pl.BlockSpec(memory_space=pl.ANY)] * 4,
-        out_specs=(pl.BlockSpec(memory_space=pltpu.VMEM),) * 2,
-        scratch_shapes=scratch,
-        compiler_params=pltpu.CompilerParams(collective_id=0, has_side_effects=True),
-    )(right_side, occupancy, region, coarse_inverse)
+        finish,
+        grid=(3,),
+        out_shape=(jax.ShapeDtypeStruct(field, f32),) * 2,
+        in_specs=[pl.BlockSpec(memory_space=pltpu.VMEM)] * 6,
+        out_specs=(block, block),
+        compiler_params=pltpu.CompilerParams(vmem_limit_bytes=16 * 1024 * 1024),
+    )(*parts)
 
 
 def solution(mesh):

time: 31.3 us -> 25.8 us (0.82)
  Pallas kernels: 27.9 us -> 25.1 us
  local copies, waits for them, and re-layouts: 2.57 us -> 0 us
    pallas_call x1 -> x2, Pallas kernels: 27.9 us -> 25.1 us  [the longest x1 23.5 us: local(): pl.pallas_call(functools.partial(kernel, nw, nn), out_shape=(V(field, f32...]
    unnamed x4 -> x0, local copies, waits for them, and re-layouts: 2.57 us -> none
where the time goes in v2:
time: 25.8 us; the launch traced here: 25.7 us
  Pallas kernels  25.1 us (97%)
  between operations  0.64 us (2%)
    pallas_call x1, Pallas kernels, local(): pl.pallas_call(functools.partial(kernel, nw, nn), out_shape=(V(field, f32...  23.5 us
    pallas_call x1, Pallas kernels, local(): pl.pallas_call(finish, grid=(3,), out_shape=(jax.ShapeDtypeStruct(field,...  1.52 us

profile of v2, /device:TPU:0, one launch (start us, length us, event | category | flops | bytes accessed | tf_op | source)
XLA Modules:
  0.0 25.7 jit_solution(16105798004047551470)
XLA Ops:
  0.6 23.5 %shard_map.59 = (f32[3,16,16,128]{3,2,1,0:T(8,128)S(1)}, f32[3,16,16,128]{3,2,1,0:T(8,128)S(1)}, f32[3,16,16,128]{3,2,1,0:T(8,128)S(1)}, f32[3,16,16,128]{3,2,1,...) custom-call(f32[3,16,16,128]{3,2,1,0:T(8,128)} %r_hbm.1, s32[16,16,128]{2,1,0:T(8,128)} %occ_hbm.1, ...), custom_call_target="tpu_custom_call" | custom-call | tf_op jit(solution)/shard_map/pallas_call | solution.py:421
  24.2 1.5 %shard_map.60 = (f32[3,16,16,128]{3,2,1,0:T(8,128)}, f32[3,16,16,128]{3,2,1,0:T(8,128)}) custom-call(f32[3,16,16,128]{3,2,1,0:T(8,128)S(1)} %get-tuple-element.8.z0_v, f32[3,16,16,128]{3,2,1,0:T(8,128)S(1)} %get-tuple-element.9.z1_v, f32[3,16,16,128]{3,2,1,0:T(8,128)S(1)} %get-tuple-element.10.r_v, f32[3,16,16,128]{3,2,1,0:T(8,128)S(1)} %get-tuple-element.11.az_v, ...), custom_call_target="tpu_custom_call" | custom-call | tf_op jit(solution)/shard_map/pallas_call | solution.py:430

commit v3 on v2

--- a/solution.py
+++ b/solution.py
@@ -386,14 +386,21 @@
         gather_wait(p, ag_send)
 
 
-def finish(z0_v, z1_v, r_v, az_v, y_v, sc_v, x_out, res_out):
-    c = pl.program_id(0)
+def finish(z0_v, z1_v, r_v, az_v, y_v, sc_v, x_out, res_out, xb, rb, sem):
     along = sc_v[0:1, 0:1]
     alpha1 = sc_v[1:2, 0:1]
     a1b = sc_v[2:3, 0:1]
-    for x in range(x_out.shape[1]):
-        x_out[0, x] = along * z0_v[c, x] + alpha1 * z1_v[c, x]
-        res_out[0, x] = r_v[c, x] - alpha1 * az_v[c, x] - a1b * y_v[c, x]
+    X = z0_v.shape[1]
+    copies = []
+    for c in range(3):
+        for x in range(X):
+            xb[c, x] = along * z0_v[c, x] + alpha1 * z1_v[c, x]
+            rb[c, x] = r_v[c, x] - alpha1 * az_v[c, x] - a1b * y_v[c, x]
+        for n, (src, dst) in enumerate(((xb, x_out), (rb, res_out))):
+            copies.append(pltpu.make_async_copy(src.at[c], dst.at[c], sem.at[n, c]))
+            copies[-1].start()
+    for copy in copies:
+        copy.wait()
 
 
 def local(nw, nn, right_side, occupancy, region, coarse_inverse):
@@ -426,13 +433,12 @@
         scratch_shapes=scratch,
         compiler_params=pltpu.CompilerParams(collective_id=0, has_side_effects=True, vmem_limit_bytes=32 * 1024 * 1024),
     )(*[pltpu.with_memory_space_constraint(a, pltpu.HBM) for a in (right_side, occupancy, region, coarse_inverse)])
-    block = pl.BlockSpec((1, X, Y, Z), lambda c: (c, 0, 0, 0))
     return pl.pallas_call(
         finish,
-        grid=(3,),
         out_shape=(jax.ShapeDtypeStruct(field, f32),) * 2,
         in_specs=[pl.BlockSpec(memory_space=pltpu.VMEM)] * 6,
-        out_specs=(block, block),
+        out_specs=(pl.BlockSpec(memory_space=pltpu.HBM),) * 2,
+        scratch_shapes=[V(field, f32), V(field, f32), pltpu.SemaphoreType.DMA((2, 3))],
         compiler_params=pltpu.CompilerParams(vmem_limit_bytes=16 * 1024 * 1024),
     )(*parts)
 

time: 25.8 us -> 25.3 us (0.981)
  Pallas kernels: 25.1 us -> 24.5 us
    pallas_call x1, Pallas kernels: 1.52 us -> 0.99 us  [local(): pl.pallas_call(finish, out_shape=(jax.ShapeDtypeStruct(field, f32),) * 2,...]
where the time goes in v3:
time: 25.3 us; the launch traced here: 25.2 us
  Pallas kernels  24.5 us (97%)
  between operations  0.64 us (3%)
    pallas_call x1, Pallas kernels, local(): pl.pallas_call(functools.partial(kernel, nw, nn), out_shape=(V(field, f32...  23.5 us
    pallas_call x1, Pallas kernels, local(): pl.pallas_call(finish, out_shape=(jax.ShapeDtypeStruct(field, f32),) * 2,...  0.99 us

profile of v3, /device:TPU:0, one launch (start us, length us, event | category | flops | bytes accessed | tf_op | source)
XLA Modules:
  0.0 25.2 jit_solution(105507030442994510)
XLA Ops:
  0.6 23.5 %shard_map.59 = (f32[3,16,16,128]{3,2,1,0:T(8,128)S(1)}, f32[3,16,16,128]{3,2,1,0:T(8,128)S(1)}, f32[3,16,16,128]{3,2,1,0:T(8,128)S(1)}, f32[3,16,16,128]{3,2,1,...) custom-call(f32[3,16,16,128]{3,2,1,0:T(8,128)} %r_hbm.1, s32[16,16,128]{2,1,0:T(8,128)} %occ_hbm.1, ...), custom_call_target="tpu_custom_call" | custom-call | tf_op jit(solution)/shard_map/pallas_call | solution.py:428
  24.2 1.0 %shard_map.60 = (f32[3,16,16,128]{3,2,1,0:T(8,128)}, f32[3,16,16,128]{3,2,1,0:T(8,128)}) custom-call(f32[3,16,16,128]{3,2,1,0:T(8,128)S(1)} %get-tuple-element.8.z0_v, f32[3,16,16,128]{3,2,1,0:T(8,128)S(1)} %get-tuple-element.9.z1_v, f32[3,16,16,128]{3,2,1,0:T(8,128)S(1)} %get-tuple-element.10.r_v, f32[3,16,16,128]{3,2,1,0:T(8,128)S(1)} %get-tuple-element.11.az_v, ...), custom_call_target="tpu_custom_call" | custom-call | tf_op jit(solution)/shard_map/pallas_call | solution.py:436
